TPU v7x, 32 devices: a whole 2x2x4 slice. The times are simulated.
32 devices in a mesh: spec: 4 (over y, core), lat: 8 (over z, x).
Axes of the slice: x: 2, y: 2, z: 4, core: 2. Of those that a mesh axis runs over, the one named last changes fastest.
Arguments:
- concentration: float32 [256, 32, 512], P('spec', 'lat'), may hold values from 0.05 to 2
- courant: float32 [32, 512], P('lat'), may hold values from -0.9 to 0.9
- rate_const: float32 [1024], replicated, may hold values from 0.005 to 0.08
- reactants: int32 [1024, 2], replicated, may hold values from 0 to 255
- products: int32 [1024, 2], replicated, may hold values from 0 to 255
- daylit: int32 [32], replicated, may hold values from 0 to 1, as said below
- block_slot: int32 [32], replicated, may hold values from 0 to 31, as said below
Outputs:
- states: float32 [256, 32, 512], P(None, 'lat', 'spec')
Inputs may be any that keep to these rules, and one draw needn't show every extreme that they name: block_slot is a permutation of the 32 rows. Grouping rows into groups of 4 in order, every row's slot lies in its own group or in the group just before or after it, and every group moves exactly one row into each neighbouring group that exists. Of the 4 slots of every group, exactly 2 are taken by rows with daylit equal to 1.
All inputs are finite; a program needn't handle non-finite values.
Results may differ from a plain program's by a relative error of at most 0.0003.
Values sent between devices are 32-bit elements; how exact they have to be, the bound alone decides.
No kernel may reach another device: no remote copies, remote signals or barrier semaphores. Data moves between devices by JAX's collectives and lax.ppermute only.
A program may use at most 64 MiB of HBM per device.

v0:
```python
import jax
import jax.numpy as jnp
from jax import lax
from jax.sharding import PartitionSpec as P

ADV_STEPS = 2
SUBSTEPS = 2


def padded_2(block, sides, width):
    for axis, dim in sides:
        count = lax.axis_size(axis)
        forward = [(i, i + 1) for i in range(count - 1)]
        backward = [(target, source) for source, target in forward]
        low = lax.ppermute(
            lax.slice_in_dim(block, block.shape[dim] - width, None, axis=dim), axis, forward
        )
        high = lax.ppermute(lax.slice_in_dim(block, 0, width, axis=dim), axis, backward)
        block = jnp.concatenate([low, block, high], axis=dim)
    return block


def passed_along(value, axis, by):
    peers = lax.axis_size(axis)
    pairs = [(i, i + by) for i in range(peers) if 0 <= i + by < peers]
    return lax.ppermute(value, axis, pairs)


def minmod(left, right):
    return 0.5 * (jnp.sign(left) + jnp.sign(right)) * jnp.minimum(jnp.abs(left), jnp.abs(right))


def sweep_rows(values, flow_rows, first_row, lat_total):
    row_count = values.shape[1]
    steps_up = values[:, 1:] - values[:, :-1]
    slopes = minmod(steps_up[:, 1:], steps_up[:, :-1])
    face_index = first_row + 2 + jnp.arange(row_count - 3, dtype=jnp.int32)
    inside = ((face_index >= 1) & (face_index <= lat_total - 1))[:, None]
    numbers = jnp.where(inside, flow_rows[2 : row_count - 1], 0.0)
    forward = jnp.maximum(numbers, 0.0) * (
        values[:, 1 : row_count - 2] + 0.5 * (1.0 - numbers) * slopes[:, 0 : row_count - 3]
    )
    backward = jnp.minimum(numbers, 0.0) * (
        values[:, 2 : row_count - 1] - 0.5 * (1.0 + numbers) * slopes[:, 1 : row_count - 2]
    )
    fluxes = forward + backward
    return values[:, 2 : row_count - 2] - (fluxes[:, 1:] - fluxes[:, :-1])


def react_cells(conc, reactants, products, rate_const):
    species_count = conc.shape[0]
    for repeat in range(SUBSTEPS):
        first_conc = jnp.take(conc, reactants[:, 0], axis=0)
        second_conc = jnp.take(conc, reactants[:, 1], axis=0)
        encounter = first_conc * second_conc
        rates = rate_const[:, None] * encounter / (1.0 + jnp.abs(encounter))
        gained = jax.ops.segment_sum(rates, products[:, 0], num_segments=species_count)
        gained = gained + jax.ops.segment_sum(rates, products[:, 1], num_segments=species_count)
        lost = jax.ops.segment_sum(rates, reactants[:, 0], num_segments=species_count)
        lost = lost + jax.ops.segment_sum(rates, reactants[:, 1], num_segments=species_count)
        conc = conc + (gained - lost)
    return conc


def on_device(concentration, courant, rate_const, reactants, products, daylit, block_slot):
    lat_rows = concentration.shape[1]
    lat_index = lax.axis_index("lat")
    lat_total = lat_rows * lax.axis_size("lat")
    base_row = lat_index * lat_rows
    values = concentration
    for repeat in range(ADV_STEPS):
        stacked = jnp.concatenate([values, courant[None]], 0)
        padded = padded_2(stacked, (("lat", 1),), 2)
        values = sweep_rows(padded[:-1], padded[-1], base_row - 2, lat_total)
    cells = lax.all_to_all(values, "spec", split_axis=2, concat_axis=0, tiled=True)
    row_ids = jnp.arange(lat_rows, dtype=jnp.int32)
    my_slots = lax.dynamic_slice_in_dim(block_slot, base_row, lat_rows)
    my_target = my_slots // lat_rows
    received = []
    for direction in (1, -1):
        chosen = jnp.sum(jnp.where(my_target == lat_index + direction, row_ids, 0))
        outgoing = lax.dynamic_index_in_dim(cells, chosen, 1, keepdims=True)
        received.append(passed_along(outgoing, "lat", direction))
    candidates = jnp.concatenate([cells] + received, 1)
    own_slots = base_row + row_ids
    matches = (block_slot[None, :] == own_slots[:, None]).astype(jnp.int32)
    all_rows = jnp.arange(block_slot.shape[0], dtype=jnp.int32)
    source = jnp.sum(matches * all_rows[None, :], axis=1)
    day_flag = jnp.sum(matches * daylit[None, :], axis=1)
    source_band = source // lat_rows
    pick_index = jnp.where(
        source_band == lat_index,
        source - base_row,
        jnp.where(source_band < lat_index, lat_rows, lat_rows + 1),
    )
    gathered = jnp.take(candidates, pick_index, axis=1)
    species_count = gathered.shape[0]
    day_count = lat_rows // 2
    ranking = jnp.cumsum(day_flag) - 1
    wanted = (day_flag[None, :] == 1) & (
        ranking[None, :] == jnp.arange(day_count, dtype=jnp.int32)[:, None]
    )
    lit_slots = jnp.sum(wanted.astype(jnp.int32) * row_ids[None, :], axis=1)
    active = jnp.take(gathered, lit_slots, axis=1)
    reacted = react_cells(
        active.reshape(species_count, -1), reactants, products, rate_const
    ).reshape(active.shape)
    states = gathered.at[:, lit_slots].set(reacted)
    return states


def solution(mesh):
    in_specs = (P("spec", "lat", None), P("lat", None), P(), P(), P(), P(), P())
    out_specs = P(None, "lat", "spec")
    return jax.shard_map(
        on_device, mesh=mesh, in_specs=in_specs, out_specs=out_specs, check_vma=False
    )
```

profile of v0, /device:TPU:0, one launch (start us, length us, event | category | flops | bytes accessed | tf_op | source)
XLA Modules:
  0.0 146.5 jit_solution(2726070398159518174)
XLA Ops:
  3.2 5.5 %collective-permute-start.1 = (f32[65,2,512]{2,0,1:T(8,128)S(1)}, f32[65,2,512]{2,0,1:T(8,128)S(1)}, u32[]{:S(2)}, u32[]{:S(2)}) collective-permute-start(f32[65,2,512]{2,0,1:T(8,128)S(1)} %copy.68), channel_id=1, source_target_pairs={{0,1},{1,2},{2,3},{3,4},{4,5},{5,6},{6,7},{8,9},{9,10},{10,11},{11... | collective-permute-start | bytes 798728 | tf_op jit(solution)/shard_map/ppermute | solution.py:15
  9.4 4.3 %collective-permute-done = f32[65,2,512]{2,0,1:T(8,128)S(1)} collective-permute-done((f32[65,2,512]{2,0,1:T(8,128)S(1)}, f32[65,2,512]{2,0,1:T(8,128)S(1)}, u32[]{:S(2)}, u32[]{:S(2)}) %collective-permute-start) | collective-permute-done | bytes 266272 | tf_op jit(solution)/shard_map/ppermute | solution.py:18
  14.2 6.0 %collective-permute-done.1 = f32[65,2,512]{2,0,1:T(8,128)S(1)} collective-permute-done((f32[65,2,512]{2,0,1:T(8,128)S(1)}, f32[65,2,512]{2,0,1:T(8,128)S(1)}, u32[]{:S(2)}, u32[]{:S(2)}) %collective-permute-start.1) | collective-permute-done | bytes 266272 | tf_op jit(solution)/shard_map/ppermute | solution.py:15
  29.0 5.0 %collective-permute-start.3 = (f32[65,2,512]{2,0,1:T(8,128)S(1)}, f32[65,2,512]{2,0,1:T(8,128)S(1)}, u32[]{:S(2)}, u32[]{:S(2)}) collective-permute-start(f32[65,2,512]{2,0,1:T(8,128)S(1)} %copy.74), channel_id=1, source_target_pairs={{0,1},{1,2},{2,3},{3,4},{4,5},{5,6},{6,7},{8,9},{9,10},{10,11},{11... | collective-permute-start | bytes 798728 | tf_op jit(solution)/shard_map/ppermute | solution.py:15
  34.8 6.0 %collective-permute-done.3 = f32[65,2,512]{2,0,1:T(8,128)S(1)} collective-permute-done((f32[65,2,512]{2,0,1:T(8,128)S(1)}, f32[65,2,512]{2,0,1:T(8,128)S(1)}, u32[]{:S(2)}, u32[]{:S(2)}) %collective-permute-start.3) | collective-permute-done | bytes 266272 | tf_op jit(solution)/shard_map/ppermute | solution.py:15
  43.6 1.8 %reshape.360 = f32[4,1,32768]{2,1,0:T(1,128)} reshape(f32[512,4,64]{2,1,0:T(4,128)S(1)} %bitcast.65) | data formatting | bytes 1048576
  45.4 3.5 %all-to-all-start = ((f32[4,1,32768]{2,1,0:T(1,128)}), f32[4,1,32768]{2,1,0:T(1,128)S(1)}, u32[]{:S(2)}, u32[]{:S(2)}) async-start(f32[4,1,32768]{2,1,0:T(1,128)} %reshape.360), calls=%async_computation | async-start | bytes 1048576 | tf_op jit(solution)/shard_map/all_to_all | solution.py:75
  49.0 8.7 %all-to-all-done = f32[4,1,32768]{2,1,0:T(1,128)S(1)} async-done(((f32[4,1,32768]{2,1,0:T(1,128)}), f32[4,1,32768]{2,1,0:T(1,128)S(1)}, u32[]{:S(2)}, u32[]{:S(2)}) %all-to-all-start) | async-done | bytes 524320 | tf_op jit(solution)/shard_map/all_to_all | solution.py:75
  58.2 2.1 %reduce = f32[4,32768]{1,0:T(4,128)S(1)} reduce(f32[4,1,32768]{2,1,0:T(1,128)S(1)} %all-to-all-done, f32[]{:T(128)} %broadcast.400), dimensions={1}, to_apply=%all_to_all.13.reduce_sub_computation | reduce | bytes 1048580 | tf_op jit(solution)/shard_map/all_to_all | solution.py:75
  62.7 5.2 %collective-permute-start.4 = (f32[256,1,128]{2,0,1:T(8,128)S(1)}, f32[256,1,128]{2,0,1:T(8,128)S(1)}, u32[]{:S(2)}, u32[]{:S(2)}) collective-permute-start(f32[256,1,128]{2,0,1:T(8,128)S(1)} %get-tuple-element.22), channel_id=1, source_target_pairs={{0,1},{1,2},{2,3},{3,4},{4,5},{5,6},{6,7},{8,9},{9,10},{10,11},{11... | collective-permute-start | bytes 393224 | tf_op jit(solution)/shard_map/ppermute | solution.py:26
  69.0 3.5 %collective-permute-done.4 = f32[256,1,128]{2,0,1:T(8,128)S(1)} collective-permute-done((f32[256,1,128]{2,0,1:T(8,128)S(1)}, f32[256,1,128]{2,0,1:T(8,128)S(1)}, u32[]{:S(2)}, u32[]{:S(2)}) %collective-permute-start.4) | collective-permute-done | bytes 131104 | tf_op jit(solution)/shard_map/ppermute | solution.py:26
  74.1 3.5 %gather_fusion.3 = f32[1024,256]{1,0:T(8,128)S(1)} fusion(f32[256,256]{1,0:T(8,128)S(1)} %broadcast_select_fusion, s32[1024]{0:T(1024)S(1)} %fusion.39), kind=kCustom, calls=%fused_computation.1.clone | custom fusion | bytes 2101248 | tf_op jit(solution)/shard_map/jit(_take)/gather | solution.py:54
  77.6 3.5 %gather_fusion.2 = f32[1024,256]{1,0:T(8,128)S(1)} fusion(f32[256,256]{1,0:T(8,128)S(1)} %broadcast_select_fusion, s32[1024]{0:T(1024)S(1)} %fusion.38), kind=kCustom, calls=%fused_computation.clone | custom fusion | bytes 2101248 | tf_op jit(solution)/shard_map/jit(_take)/gather | solution.py:53
  81.1 1.7 %add_divide_fusion.1 = f32[1024,256]{1,0:T(8,128)} fusion(f32[1024,256]{1,0:T(8,128)S(1)} %gather_fusion.3, f32[1024,256]{1,0:T(8,128)S(1)} %gather_fusion.2, f32[1024]{0:T(1024)S(1)} %copy-done.2, pred[1024]{0:T(1024)(128)(4,1)S(1)} %get-tuple-element.28, pred[1024]{0:T(1024)(128)(4,1)S(1)} %get-tuple-element.29), kind=kLoop, calls=%fused_computation.48 | loop fusion | flops 1835008 | bytes 3151872 | tf_op jit(solution)/shard_map/div | solution.py:56
  82.8 6.6 %scatter_custom_fusion.2 = f32[256,256]{1,0:T(8,128)S(1)} fusion(s32[1024]{0:T(1024)S(1)} %bitcast.85, f32[1024,256]{1,0:T(8,128)} %add_divide_fusion.1, f32[]{:T(128)} %constant.99.clone.1), kind=kCustom, calls=%fused_computation.77 | custom fusion | flops 262144 | bytes 262656 | tf_op jit(solution)/shard_map/scatter-add | solution.py:59
  89.4 6.6 %scatter_custom_fusion.3 = f32[256,256]{1,0:T(8,128)S(1)} fusion(s32[1024]{0:T(1024)S(1)} %bitcast.81, f32[1024,256]{1,0:T(8,128)} %add_divide_fusion.1, f32[]{:T(128)} %constant.99.clone.1), kind=kCustom, calls=%fused_computation.75 | custom fusion | flops 262144 | bytes 262656 | tf_op jit(solution)/shard_map/scatter-add | solution.py:60
  96.0 6.6 %scatter_custom_fusion = f32[256,256]{1,0:T(8,128)S(1)} fusion(s32[1024]{0:T(1024)S(1)} %bitcast.89, f32[1024,256]{1,0:T(8,128)} %add_divide_fusion.1, f32[]{:T(128)} %constant.99.clone.1), kind=kCustom, calls=%fused_computation.81 | custom fusion | flops 262144 | bytes 262656 | tf_op jit(solution)/shard_map/scatter-add | solution.py:57
  102.6 6.8 %scatter_custom_fusion.1 = f32[256,256]{1,0:T(8,128)S(1)} fusion(s32[1024]{0:T(1024)S(1)} %bitcast.87, f32[1024,256]{1,0:T(8,128)} %add_divide_fusion.1, f32[]{:T(128)} %constant.99.clone.1), kind=kCustom, calls=%fused_computation.79 | custom fusion | flops 262144 | bytes 262656 | tf_op jit(solution)/shard_map/scatter-add | solution.py:58
  109.5 3.5 %gather_fusion.5 = f32[1024,256]{1,0:T(8,128)S(1)} fusion(f32[256,256]{1,0:T(8,128)S(1)} %subtract_add_fusion, s32[1024]{0:T(1024)S(1)} %fusion.39), kind=kCustom, calls=%fused_computation.3.clone | custom fusion | bytes 2101248 | tf_op jit(solution)/shard_map/jit(_take)/gather | solution.py:54
  113.0 3.5 %gather_fusion.4 = f32[1024,256]{1,0:T(8,128)S(1)} fusion(f32[256,256]{1,0:T(8,128)S(1)} %subtract_add_fusion, s32[1024]{0:T(1024)S(1)} %fusion.38), kind=kCustom, calls=%fused_computation.2.clone | custom fusion | bytes 2101248 | tf_op jit(solution)/shard_map/jit(_take)/gather | solution.py:53
  118.2 6.6 %scatter_custom_fusion.6 = f32[256,256]{1,0:T(8,128)S(1)} fusion(s32[1024]{0:T(1024)S(1)} %bitcast.86, f32[1024,256]{1,0:T(8,128)} %add_divide_fusion, f32[]{:T(128)} %constant.99.clone.1), kind=kCustom, calls=%fused_computation.69 | custom fusion | flops 262144 | bytes 262656 | tf_op jit(solution)/shard_map/scatter-add | solution.py:59
  124.8 6.6 %scatter_custom_fusion.7 = f32[256,256]{1,0:T(8,128)S(1)} fusion(s32[1024]{0:T(1024)S(1)} %bitcast.82, f32[1024,256]{1,0:T(8,128)} %add_divide_fusion, f32[]{:T(128)} %constant.99.clone.1), kind=kCustom, calls=%fused_computation.67 | custom fusion | flops 262144 | bytes 262656 | tf_op jit(solution)/shard_map/scatter-add | solution.py:60
  131.4 6.6 %scatter_custom_fusion.4 = f32[256,256]{1,0:T(8,128)S(1)} fusion(s32[1024]{0:T(1024)S(1)} %bitcast.90, f32[1024,256]{1,0:T(8,128)} %add_divide_fusion, f32[]{:T(128)} %constant.99.clone.1), kind=kCustom, calls=%fused_computation.73 | custom fusion | flops 262144 | bytes 262656 | tf_op jit(solution)/shard_map/scatter-add | solution.py:57
  138.0 6.6 %scatter_custom_fusion.5 = f32[256,256]{1,0:T(8,128)S(1)} fusion(s32[1024]{0:T(1024)S(1)} %bitcast.88, f32[1024,256]{1,0:T(8,128)} %add_divide_fusion, f32[]{:T(128)} %constant.99.clone.1), kind=kCustom, calls=%fused_computation.71 | custom fusion | flops 262144 | bytes 262656 | tf_op jit(solution)/shard_map/scatter-add | solution.py:58
  (80 shorter events, 21.6 us)
Async XLA Ops:
  0.0 8.7 %copy-start.5 = (s32[32]{0:T(128)S(1)}, s32[32]{0:T(128)}, u32[]{:S(2)}) copy-start(s32[32]{0:T(128)} %param.15) | copy-start | bytes 388
  0.0 8.7 %copy-start.6 = (s32[32]{0:T(128)S(1)}, s32[32]{0:T(128)}, u32[]{:S(2)}) copy-start(s32[32]{0:T(128)} %param.14) | copy-start | bytes 388
  0.0 9.0 %copy-start.3 = (s32[1024,2]{0,1:T(2,128)S(1)}, s32[1024,2]{0,1:T(2,128)}, u32[]{:S(2)}) copy-start(s32[1024,2]{0,1:T(2,128)} %param.12) | copy-start | bytes 24580
  1.6 12.3 %copy-start = (f32[64,4,512]{2,1,0:T(4,128)S(1)}, f32[64,4,512]{2,1,0:T(4,128)}, u32[]{:S(2)}) copy-start(f32[64,4,512]{2,1,0:T(4,128)} %param.9) | copy-start | bytes 1572868
  1.6 12.3 %copy-start.1 = (f32[4,512]{1,0:T(4,128)S(1)}, f32[4,512]{1,0:T(4,128)}, u32[]{:S(2)}) copy-start(f32[4,512]{1,0:T(4,128)} %param.10) | copy-start | bytes 24580
  1.7 12.0 %collective-permute-start = (f32[65,2,512]{2,0,1:T(8,128)S(1)}, f32[65,2,512]{2,0,1:T(8,128)S(1)}, u32[]{:S(2)}, u32[]{:S(2)}) collective-permute-start(f32[65,2,512]{2,0,1:T(8,128)S(1)} %copy.66), channel_id=1, source_target_pairs={{1,0},{2,1},{3,2},{4,3},{5,4},{6,5},{7,6},{9,8},{10,9},{11,10},{12... | collective-permute-start | bytes 798728 | tf_op jit(solution)/shard_map/ppermute | solution.py:18
  3.2 17.0 %collective-permute-start.1 = (f32[65,2,512]{2,0,1:T(8,128)S(1)}, f32[65,2,512]{2,0,1:T(8,128)S(1)}, u32[]{:S(2)}, u32[]{:S(2)}) collective-permute-start(f32[65,2,512]{2,0,1:T(8,128)S(1)} %copy.68), channel_id=1, source_target_pairs={{0,1},{1,2},{2,3},{3,4},{4,5},{5,6},{6,7},{8,9},{9,10},{10,11},{11... | collective-permute-start | bytes 798728 | tf_op jit(solution)/shard_map/ppermute | solution.py:15
  22.8 11.6 %collective-permute-start.2 = (f32[65,2,512]{2,0,1:T(8,128)S(1)}, f32[65,2,512]{2,0,1:T(8,128)S(1)}, u32[]{:S(2)}, u32[]{:S(2)}) collective-permute-start(f32[65,2,512]{2,0,1:T(8,128)S(1)} %copy.72), channel_id=1, source_target_pairs={{1,0},{2,1},{3,2},{4,3},{5,4},{6,5},{7,6},{9,8},{10,9},{11,10},{12... | collective-permute-start | bytes 798728 | tf_op jit(solution)/shard_map/ppermute | solution.py:18
  29.0 11.9 %collective-permute-start.3 = (f32[65,2,512]{2,0,1:T(8,128)S(1)}, f32[65,2,512]{2,0,1:T(8,128)S(1)}, u32[]{:S(2)}, u32[]{:S(2)}) collective-permute-start(f32[65,2,512]{2,0,1:T(8,128)S(1)} %copy.74), channel_id=1, source_target_pairs={{0,1},{1,2},{2,3},{3,4},{4,5},{5,6},{6,7},{8,9},{9,10},{10,11},{11... | collective-permute-start | bytes 798728 | tf_op jit(solution)/shard_map/ppermute | solution.py:15
  43.6 5.3 %copy-start.4 = (s32[1024,2]{0,1:T(2,128)S(1)}, s32[1024,2]{0,1:T(2,128)}, u32[]{:S(2)}) copy-start(s32[1024,2]{0,1:T(2,128)} %param.13) | copy-start | bytes 24580
  45.4 12.3 %all-to-all-start = ((f32[4,1,32768]{2,1,0:T(1,128)}), f32[4,1,32768]{2,1,0:T(1,128)S(1)}, u32[]{:S(2)}, u32[]{:S(2)}) async-start(f32[4,1,32768]{2,1,0:T(1,128)} %reshape.360), calls=%async_computation | async-start | bytes 1048576 | tf_op jit(solution)/shard_map/all_to_all | solution.py:75
  61.4 7.6 %collective-permute-start.5 = (f32[256,1,128]{2,0,1:T(8,128)S(1)}, f32[256,1,128]{2,0,1:T(8,128)S(1)}, u32[]{:S(2)}, u32[]{:S(2)}) collective-permute-start(f32[256,1,128]{2,0,1:T(8,128)S(1)} %get-tuple-element.23), channel_id=1, source_target_pairs={{1,0},{2,1},{3,2},{4,3},{5,4},{6,5},{7,6},{9,8},{10,9},{11,10},{12... | collective-permute-start | bytes 393224 | tf_op jit(solution)/shard_map/ppermute | solution.py:26
  62.7 9.7 %collective-permute-start.4 = (f32[256,1,128]{2,0,1:T(8,128)S(1)}, f32[256,1,128]{2,0,1:T(8,128)S(1)}, u32[]{:S(2)}, u32[]{:S(2)}) collective-permute-start(f32[256,1,128]{2,0,1:T(8,128)S(1)} %get-tuple-element.22), channel_id=1, source_target_pairs={{0,1},{1,2},{2,3},{3,4},{4,5},{5,6},{6,7},{8,9},{9,10},{10,11},{11... | collective-permute-start | bytes 393224 | tf_op jit(solution)/shard_map/ppermute | solution.py:26
  77.6 3.5 %copy-start.2 = (f32[1024]{0:T(1024)S(1)}, f32[1024]{0:T(1024)}, u32[]{:S(2)}) copy-start(f32[1024]{0:T(1024)} %param.11) | copy-start | bytes 12292
where the time goes:
time: 147 us; the launch traced here: 146 us
  other arithmetic  66.8 us (45%)
  waiting for transfers between devices  29.9 us (20%)
  starting transfers between devices  23.2 us (16%)
  local copies, waits for them, and re-layouts  22 us (15%)
  between operations  4.58 us (3%)
    scatter-add x2, other arithmetic, react_cells(): jax.ops.segment_sum(rates, products[:, 1], num_segments=species_count)  13.4 us
    scatter-add x2, other arithmetic, react_cells(): jax.ops.segment_sum(rates, reactants[:, 1], num_segments=species_count)  13.2 us
    scatter-add x2, other arithmetic, react_cells(): jax.ops.segment_sum(rates, products[:, 0], num_segments=species_count)  13.2 us
    scatter-add x2, other arithmetic, react_cells(): jax.ops.segment_sum(rates, reactants[:, 0], num_segments=species_count)  13.2 us
    ppermute x2, waiting for transfers between devices, padded_2(): lax.ppermute(lax.slice_in_dim(block, block.shape[dim] - width, None, axis...  12.1 us
    ppermute x2, starting transfers between devices, padded_2(): lax.ppermute(lax.slice_in_dim(block, block.shape[dim] - width, None, axis...  10.6 us
    all_to_all x1, waiting for transfers between devices, on_device(): lax.all_to_all(values, 'spec', split_axis=2, concat_axis=0, tiled=True)  8.69 us
    gather x2, local copies, waits for them, and re-layouts, react_cells(): first_conc = jnp.take(conc, reactants[:, 0], axis=0)  6.93 us
  transfers between devices with their start and end apart: 7, of which 7 were waited for; matrix products, arithmetic and copies ran while one was open for 2% of the time, Pallas kernels for 0%

commit v1 on v0

--- a/solution.py
+++ b/solution.py
@@ -72,7 +72,10 @@
         stacked = jnp.concatenate([values, courant[None]], 0)
         padded = padded_2(stacked, (("lat", 1),), 2)
         values = sweep_rows(padded[:-1], padded[-1], base_row - 2, lat_total)
-    cells = lax.all_to_all(values, "spec", split_axis=2, concat_axis=0, tiled=True)
+    cells = jnp.concatenate(
+        lax.all_to_all(jnp.stack(jnp.split(values, lax.axis_size("spec"), axis=2)), "spec", 0, 0),
+        axis=0,
+    )
     row_ids = jnp.arange(lat_rows, dtype=jnp.int32)
     my_slots = lax.dynamic_slice_in_dim(block_slot, base_row, lat_rows)
     my_target = my_slots // lat_rows

time: 147 us -> 142 us (0.966)
  local copies, waits for them, and re-layouts: 22 us -> 18.4 us
    unnamed x16 -> x14, local copies, waits for them, and re-layouts: 2.52 us -> 0.04 us
    all_to_all x1 -> x0, other arithmetic: 2.14 us -> none  [on_device(): lax.all_to_all(values, 'spec', split_axis=2, concat_axis=0, tiled=True)]
where the time goes in v1:
time: 142 us
  other arithmetic  65.7 us (46%)
  waiting for transfers between devices  30.1 us (21%)
  starting transfers between devices  23.1 us (16%)
  local copies, waits for them, and re-layouts  18.4 us (13%)
  between operations  4.57 us (3%)
    scatter-add x2, other arithmetic, react_cells(): jax.ops.segment_sum(rates, reactants[:, 0], num_segments=species_count)  13.6 us
    scatter-add x2, other arithmetic, react_cells(): jax.ops.segment_sum(rates, reactants[:, 1], num_segments=species_count)  13.2 us
    scatter-add x2, other arithmetic, react_cells(): jax.ops.segment_sum(rates, products[:, 0], num_segments=species_count)  13.2 us
    scatter-add x2, other arithmetic, react_cells(): jax.ops.segment_sum(rates, products[:, 1], num_segments=species_count)  13.2 us
    ppermute x2, waiting for transfers between devices, padded_2(): lax.ppermute(lax.slice_in_dim(block, block.shape[dim] - width, None, axis...  12.1 us
    ppermute x2, starting transfers between devices, padded_2(): lax.ppermute(lax.slice_in_dim(block, block.shape[dim] - width, None, axis...  10.6 us
    all_to_all x1, waiting for transfers between devices, on_device(): lax.all_to_all(jnp.stack(jnp.split(values, lax.axis_size('spec'), axis=2)...  8.69 us
    gather x2, local copies, waits for them, and re-layouts, react_cells(): second_conc = jnp.take(conc, reactants[:, 1], axis=0)  6.93 us
  transfers between devices with their start and end apart: 7, of which 7 were waited for; matrix products, arithmetic and copies ran while one was open for 2% of the time, Pallas kernels for 0%

profile of v1, /device:TPU:0, one launch (start us, length us, event | category | flops | bytes accessed | tf_op | source)
XLA Modules:
  0.0 141.8 jit_solution(613984095993490954)
XLA Ops:
  0.0 1.6 %pad_maximum_fusion.9 = (f32[65,2,512]{2,1,0:T(2,128)S(1)}, f32[65,2,512]{2,1,0:T(2,128)S(1)}) fusion(f32[1,4,512]{2,1,0:T(4,128)} %bitcast.71, f32[64,4,512]{2,1,0:T(4,128)} %param.9), kind=kLoop, calls=%fused_computation.62 | loop fusion | flops 133120 | bytes 1064960 | tf_op jit(solution)/shard_map/concatenate | solution.py:72
  3.2 5.5 %collective-permute-start.1 = (f32[65,2,512]{2,0,1:T(8,128)S(1)}, f32[65,2,512]{2,0,1:T(8,128)S(1)}, u32[]{:S(2)}, u32[]{:S(2)}) collective-permute-start(f32[65,2,512]{2,0,1:T(8,128)S(1)} %copy.45), channel_id=1, source_target_pairs={{0,1},{1,2},{2,3},{3,4},{4,5},{5,6},{6,7},{8,9},{9,10},{10,11},{11... | collective-permute-start | bytes 798728 | tf_op jit(solution)/shard_map/ppermute | solution.py:15
  9.4 4.3 %collective-permute-done = f32[65,2,512]{2,0,1:T(8,128)S(1)} collective-permute-done((f32[65,2,512]{2,0,1:T(8,128)S(1)}, f32[65,2,512]{2,0,1:T(8,128)S(1)}, u32[]{:S(2)}, u32[]{:S(2)}) %collective-permute-start) | collective-permute-done | bytes 266272 | tf_op jit(solution)/shard_map/ppermute | solution.py:18
  14.2 6.0 %collective-permute-done.1 = f32[65,2,512]{2,0,1:T(8,128)S(1)} collective-permute-done((f32[65,2,512]{2,0,1:T(8,128)S(1)}, f32[65,2,512]{2,0,1:T(8,128)S(1)}, u32[]{:S(2)}, u32[]{:S(2)}) %collective-permute-start.1) | collective-permute-done | bytes 266272 | tf_op jit(solution)/shard_map/ppermute | solution.py:15
  29.0 5.0 %collective-permute-start.3 = (f32[65,2,512]{2,0,1:T(8,128)S(1)}, f32[65,2,512]{2,0,1:T(8,128)S(1)}, u32[]{:S(2)}, u32[]{:S(2)}) collective-permute-start(f32[65,2,512]{2,0,1:T(8,128)S(1)} %copy.51), channel_id=1, source_target_pairs={{0,1},{1,2},{2,3},{3,4},{4,5},{5,6},{6,7},{8,9},{9,10},{10,11},{11... | collective-permute-start | bytes 798728 | tf_op jit(solution)/shard_map/ppermute | solution.py:15
  34.8 6.0 %collective-permute-done.3 = f32[65,2,512]{2,0,1:T(8,128)S(1)} collective-permute-done((f32[65,2,512]{2,0,1:T(8,128)S(1)}, f32[65,2,512]{2,0,1:T(8,128)S(1)}, u32[]{:S(2)}, u32[]{:S(2)}) %collective-permute-start.3) | collective-permute-done | bytes 266272 | tf_op jit(solution)/shard_map/ppermute | solution.py:15
  44.2 3.5 %all-to-all-start = ((f32[4,64,4,128]{3,2,1,0:T(4,128)}), f32[4,64,4,128]{3,2,1,0:T(4,128)S(1)}, u32[]{:S(2)}, u32[]{:S(2)}) async-start(f32[4,64,4,128]{3,2,1,0:T(4,128)} %pad_maximum_fusion.7), calls=%async_computation | async-start | bytes 1048576 | tf_op jit(solution)/shard_map/all_to_all | solution.py:76
  47.8 8.7 %all-to-all-done = f32[4,64,4,128]{3,2,1,0:T(4,128)S(1)} async-done(((f32[4,64,4,128]{3,2,1,0:T(4,128)}), f32[4,64,4,128]{3,2,1,0:T(4,128)S(1)}, u32[]{:S(2)}, u32[]{:S(2)}) %all-to-all-start) | async-done | bytes 524320 | tf_op jit(solution)/shard_map/all_to_all | solution.py:76
  57.9 5.0 %collective-permute-start.4 = (f32[256,1,128]{2,0,1:T(8,128)S(1)}, f32[256,1,128]{2,0,1:T(8,128)S(1)}, u32[]{:S(2)}, u32[]{:S(2)}) collective-permute-start(f32[256,1,128]{2,0,1:T(8,128)S(1)} %get-tuple-element.22), channel_id=1, source_target_pairs={{0,1},{1,2},{2,3},{3,4},{4,5},{5,6},{6,7},{8,9},{9,10},{10,11},{11... | collective-permute-start | bytes 393224 | tf_op jit(solution)/shard_map/ppermute | solution.py:26
  64.2 3.5 %collective-permute-done.4 = f32[256,1,128]{2,0,1:T(8,128)S(1)} collective-permute-done((f32[256,1,128]{2,0,1:T(8,128)S(1)}, f32[256,1,128]{2,0,1:T(8,128)S(1)}, u32[]{:S(2)}, u32[]{:S(2)}) %collective-permute-start.4) | collective-permute-done | bytes 131104 | tf_op jit(solution)/shard_map/ppermute | solution.py:26
  69.3 3.5 %gather_fusion.3 = f32[1024,256]{1,0:T(8,128)S(1)} fusion(f32[256,256]{1,0:T(8,128)S(1)} %broadcast_select_fusion, s32[1024]{0:T(1024)S(1)} %fusion.39), kind=kCustom, calls=%fused_computation.1.clone | custom fusion | bytes 2101248 | tf_op jit(solution)/shard_map/jit(_take)/gather | solution.py:54
  72.7 3.5 %gather_fusion.2 = f32[1024,256]{1,0:T(8,128)S(1)} fusion(f32[256,256]{1,0:T(8,128)S(1)} %broadcast_select_fusion, s32[1024]{0:T(1024)S(1)} %fusion.38), kind=kCustom, calls=%fused_computation.clone | custom fusion | bytes 2101248 | tf_op jit(solution)/shard_map/jit(_take)/gather | solution.py:53
  76.2 1.7 %add_divide_fusion.1 = f32[1024,256]{1,0:T(8,128)} fusion(f32[1024,256]{1,0:T(8,128)S(1)} %gather_fusion.3, f32[1024,256]{1,0:T(8,128)S(1)} %gather_fusion.2, f32[1024]{0:T(1024)S(1)} %copy-done.2, pred[1024]{0:T(1024)(128)(4,1)S(1)} %get-tuple-element.32, pred[1024]{0:T(1024)(128)(4,1)S(1)} %get-tuple-element.33), kind=kLoop, calls=%fused_computation.48 | loop fusion | flops 1835008 | bytes 3151872 | tf_op jit(solution)/shard_map/div | solution.py:56
  77.9 6.8 %scatter_custom_fusion.2 = f32[256,256]{1,0:T(8,128)S(1)} fusion(s32[1024]{0:T(1024)S(1)} %bitcast.85, f32[1024,256]{1,0:T(8,128)} %add_divide_fusion.1, f32[]{:T(128)} %constant.99.clone.1), kind=kCustom, calls=%fused_computation.82 | custom fusion | flops 262144 | bytes 262656 | tf_op jit(solution)/shard_map/scatter-add | solution.py:59
  84.7 6.6 %scatter_custom_fusion.3 = f32[256,256]{1,0:T(8,128)S(1)} fusion(s32[1024]{0:T(1024)S(1)} %bitcast.81, f32[1024,256]{1,0:T(8,128)} %add_divide_fusion.1, f32[]{:T(128)} %constant.99.clone.1), kind=kCustom, calls=%fused_computation.80 | custom fusion | flops 262144 | bytes 262656 | tf_op jit(solution)/shard_map/scatter-add | solution.py:60
  91.3 6.6 %scatter_custom_fusion = f32[256,256]{1,0:T(8,128)S(1)} fusion(s32[1024]{0:T(1024)S(1)} %bitcast.89, f32[1024,256]{1,0:T(8,128)} %add_divide_fusion.1, f32[]{:T(128)} %constant.99.clone.1), kind=kCustom, calls=%fused_computation.86 | custom fusion | flops 262144 | bytes 262656 | tf_op jit(solution)/shard_map/scatter-add | solution.py:57
  97.9 6.6 %scatter_custom_fusion.1 = f32[256,256]{1,0:T(8,128)S(1)} fusion(s32[1024]{0:T(1024)S(1)} %bitcast.87, f32[1024,256]{1,0:T(8,128)} %add_divide_fusion.1, f32[]{:T(128)} %constant.99.clone.1), kind=kCustom, calls=%fused_computation.84 | custom fusion | flops 262144 | bytes 262656 | tf_op jit(solution)/shard_map/scatter-add | solution.py:58
  104.6 3.5 %gather_fusion.5 = f32[1024,256]{1,0:T(8,128)S(1)} fusion(f32[256,256]{1,0:T(8,128)S(1)} %subtract_add_fusion, s32[1024]{0:T(1024)S(1)} %fusion.39), kind=kCustom, calls=%fused_computation.3.clone | custom fusion | bytes 2101248 | tf_op jit(solution)/shard_map/jit(_take)/gather | solution.py:54
  108.1 3.5 %gather_fusion.4 = f32[1024,256]{1,0:T(8,128)S(1)} fusion(f32[256,256]{1,0:T(8,128)S(1)} %subtract_add_fusion, s32[1024]{0:T(1024)S(1)} %fusion.38), kind=kCustom, calls=%fused_computation.2.clone | custom fusion | bytes 2101248 | tf_op jit(solution)/shard_map/jit(_take)/gather | solution.py:53
  111.6 1.7 %add_divide_fusion = f32[1024,256]{1,0:T(8,128)} fusion(f32[1024,256]{1,0:T(8,128)S(1)} %gather_fusion.5, f32[1024,256]{1,0:T(8,128)S(1)} %gather_fusion.4, f32[1024]{0:T(1024)S(1)} %copy-done.2, pred[1024]{0:T(1024)(128)(4,1)S(1)} %get-tuple-element.32, pred[1024]{0:T(1024)(128)(4,1)S(1)} %get-tuple-element.33), kind=kLoop, calls=%fused_computation.47 | loop fusion | flops 1835008 | bytes 3151872 | tf_op jit(solution)/shard_map/div | solution.py:56
  113.3 6.8 %scatter_custom_fusion.6 = f32[256,256]{1,0:T(8,128)S(1)} fusion(s32[1024]{0:T(1024)S(1)} %bitcast.86, f32[1024,256]{1,0:T(8,128)} %add_divide_fusion, f32[]{:T(128)} %constant.99.clone.1), kind=kCustom, calls=%fused_computation.74 | custom fusion | flops 262144 | bytes 262656 | tf_op jit(solution)/shard_map/scatter-add | solution.py:59
  120.1 6.6 %scatter_custom_fusion.7 = f32[256,256]{1,0:T(8,128)S(1)} fusion(s32[1024]{0:T(1024)S(1)} %bitcast.82, f32[1024,256]{1,0:T(8,128)} %add_divide_fusion, f32[]{:T(128)} %constant.99.clone.1), kind=kCustom, calls=%fused_computation.72 | custom fusion | flops 262144 | bytes 262656 | tf_op jit(solution)/shard_map/scatter-add | solution.py:60
  126.7 6.6 %scatter_custom_fusion.4 = f32[256,256]{1,0:T(8,128)S(1)} fusion(s32[1024]{0:T(1024)S(1)} %bitcast.90, f32[1024,256]{1,0:T(8,128)} %add_divide_fusion, f32[]{:T(128)} %constant.99.clone.1), kind=kCustom, calls=%fused_computation.78 | custom fusion | flops 262144 | bytes 262656 | tf_op jit(solution)/shard_map/scatter-add | solution.py:57
  133.3 6.6 %scatter_custom_fusion.5 = f32[256,256]{1,0:T(8,128)S(1)} fusion(s32[1024]{0:T(1024)S(1)} %bitcast.88, f32[1024,256]{1,0:T(8,128)} %add_divide_fusion, f32[]{:T(128)} %constant.99.clone.1), kind=kCustom, calls=%fused_computation.76 | custom fusion | flops 262144 | bytes 262656 | tf_op jit(solution)/shard_map/scatter-add | solution.py:58
  (77 shorter events, 17.6 us)
Async XLA Ops:
  0.0 8.7 %copy-start.5 = (s32[32]{0:T(128)S(1)}, s32[32]{0:T(128)}, u32[]{:S(2)}) copy-start(s32[32]{0:T(128)} %param.15) | copy-start | bytes 388
  0.0 8.7 %copy-start.6 = (s32[32]{0:T(128)S(1)}, s32[32]{0:T(128)}, u32[]{:S(2)}) copy-start(s32[32]{0:T(128)} %param.14) | copy-start | bytes 388
  0.0 9.0 %copy-start.3 = (s32[1024,2]{0,1:T(2,128)S(1)}, s32[1024,2]{0,1:T(2,128)}, u32[]{:S(2)}) copy-start(s32[1024,2]{0,1:T(2,128)} %param.12) | copy-start | bytes 24580
  1.6 12.3 %copy-start = (f32[64,4,512]{2,1,0:T(4,128)S(1)}, f32[64,4,512]{2,1,0:T(4,128)}, u32[]{:S(2)}) copy-start(f32[64,4,512]{2,1,0:T(4,128)} %param.9) | copy-start | bytes 1572868
  1.6 12.3 %copy-start.1 = (f32[4,512]{1,0:T(4,128)S(1)}, f32[4,512]{1,0:T(4,128)}, u32[]{:S(2)}) copy-start(f32[4,512]{1,0:T(4,128)} %param.10) | copy-start | bytes 24580
  1.7 12.0 %collective-permute-start = (f32[65,2,512]{2,0,1:T(8,128)S(1)}, f32[65,2,512]{2,0,1:T(8,128)S(1)}, u32[]{:S(2)}, u32[]{:S(2)}) collective-permute-start(f32[65,2,512]{2,0,1:T(8,128)S(1)} %copy.43), channel_id=1, source_target_pairs={{1,0},{2,1},{3,2},{4,3},{5,4},{6,5},{7,6},{9,8},{10,9},{11,10},{12... | collective-permute-start | bytes 798728 | tf_op jit(solution)/shard_map/ppermute | solution.py:18
  3.2 17.0 %collective-permute-start.1 = (f32[65,2,512]{2,0,1:T(8,128)S(1)}, f32[65,2,512]{2,0,1:T(8,128)S(1)}, u32[]{:S(2)}, u32[]{:S(2)}) collective-permute-start(f32[65,2,512]{2,0,1:T(8,128)S(1)} %copy.45), channel_id=1, source_target_pairs={{0,1},{1,2},{2,3},{3,4},{4,5},{5,6},{6,7},{8,9},{9,10},{10,11},{11... | collective-permute-start | bytes 798728 | tf_op jit(solution)/shard_map/ppermute | solution.py:15
  22.8 11.6 %collective-permute-start.2 = (f32[65,2,512]{2,0,1:T(8,128)S(1)}, f32[65,2,512]{2,0,1:T(8,128)S(1)}, u32[]{:S(2)}, u32[]{:S(2)}) collective-permute-start(f32[65,2,512]{2,0,1:T(8,128)S(1)} %copy.49), channel_id=1, source_target_pairs={{1,0},{2,1},{3,2},{4,3},{5,4},{6,5},{7,6},{9,8},{10,9},{11,10},{12... | collective-permute-start | bytes 798728 | tf_op jit(solution)/shard_map/ppermute | solution.py:18
  29.0 11.9 %collective-permute-start.3 = (f32[65,2,512]{2,0,1:T(8,128)S(1)}, f32[65,2,512]{2,0,1:T(8,128)S(1)}, u32[]{:S(2)}, u32[]{:S(2)}) collective-permute-start(f32[65,2,512]{2,0,1:T(8,128)S(1)} %copy.51), channel_id=1, source_target_pairs={{0,1},{1,2},{2,3},{3,4},{4,5},{5,6},{6,7},{8,9},{9,10},{10,11},{11... | collective-permute-start | bytes 798728 | tf_op jit(solution)/shard_map/ppermute | solution.py:15
  43.3 4.5 %copy-start.4 = (s32[1024,2]{0,1:T(2,128)S(1)}, s32[1024,2]{0,1:T(2,128)}, u32[]{:S(2)}) copy-start(s32[1024,2]{0,1:T(2,128)} %param.13) | copy-start | bytes 24580
  44.2 12.3 %all-to-all-start = ((f32[4,64,4,128]{3,2,1,0:T(4,128)}), f32[4,64,4,128]{3,2,1,0:T(4,128)S(1)}, u32[]{:S(2)}, u32[]{:S(2)}) async-start(f32[4,64,4,128]{3,2,1,0:T(4,128)} %pad_maximum_fusion.7), calls=%async_computation | async-start | bytes 1048576 | tf_op jit(solution)/shard_map/all_to_all | solution.py:76
  56.6 7.6 %collective-permute-start.5 = (f32[256,1,128]{2,0,1:T(8,128)S(1)}, f32[256,1,128]{2,0,1:T(8,128)S(1)}, u32[]{:S(2)}, u32[]{:S(2)}) collective-permute-start(f32[256,1,128]{2,0,1:T(8,128)S(1)} %get-tuple-element.23), channel_id=1, source_target_pairs={{1,0},{2,1},{3,2},{4,3},{5,4},{6,5},{7,6},{9,8},{10,9},{11,10},{12... | collective-permute-start | bytes 393224 | tf_op jit(solution)/shard_map/ppermute | solution.py:26
  57.9 9.7 %collective-permute-start.4 = (f32[256,1,128]{2,0,1:T(8,128)S(1)}, f32[256,1,128]{2,0,1:T(8,128)S(1)}, u32[]{:S(2)}, u32[]{:S(2)}) collective-permute-start(f32[256,1,128]{2,0,1:T(8,128)S(1)} %get-tuple-element.22), channel_id=1, source_target_pairs={{0,1},{1,2},{2,3},{3,4},{4,5},{5,6},{6,7},{8,9},{9,10},{10,11},{11... | collective-permute-start | bytes 393224 | tf_op jit(solution)/shard_map/ppermute | solution.py:26
  72.7 3.5 %copy-start.2 = (f32[1024]{0:T(1024)S(1)}, f32[1024]{0:T(1024)}, u32[]{:S(2)}) copy-start(f32[1024]{0:T(1024)} %param.11) | copy-start | bytes 12292
